TPU v7x, 32 devices: a whole 2x2x4 slice. The times are simulated.
32 devices in a mesh: pipe: 8 (over z, x), expert: 4 (over y, core).
Axes of the slice: x: 2, y: 2, z: 4, core: 2. Of those that a mesh axis runs over, the one named last changes fastest.
Arguments:
- forward_in: bfloat16 [8, 256, 3584], P('pipe', 'expert'), may hold values from -6 to 6
- forward_ids: int32 [8, 256, 1], P('pipe', 'expert'), may hold values from 0 to 1, as said below
- forward_gates: float32 [8, 256, 1], P('pipe', 'expert'), may hold values from 0.4 to 1
- grad_in: bfloat16 [8, 256, 3584], P('pipe', 'expert'), may hold values from -6 to 6
- grad_ids: int32 [8, 256, 1], P('pipe', 'expert'), may hold values from 0 to 1, as said below
- grad_gates: float32 [8, 256, 1], P('pipe', 'expert'), may hold values from 0.4 to 1
- saved_input: bfloat16 [8, 256, 3584], P('pipe', 'expert'), may hold values from -6 to 6
- saved_acts: bfloat16 [8, 4, 128, 1024], P('pipe', 'expert'), may hold values from -8 to 8
- norm_gain: float32 [8, 3584], P('pipe'), may hold values from 0.1 to 1.9
- weight_in: bfloat16 [4, 3584, 1024], P('expert'), may hold values from -0.09375 to 0.09375
- weight_out: bfloat16 [4, 512, 3584], P('expert'), may hold values from -0.1875 to 0.1875
Outputs:
- forward_out: bfloat16 [8, 256, 3584], P('pipe', 'expert')
- grad_out: bfloat16 [8, 256, 3584], P('pipe', 'expert')
Inputs may be any that keep to these rules, and one draw needn't show every extreme that they name: `forward_ids`: A token's 1 ids are distinct; for each section, the 64 tokens of one device name every expert exactly 32 times. `grad_ids`: A token's 1 ids are distinct; for each section, the 64 tokens of one device name every expert exactly 32 times.
All inputs are finite; a program needn't handle non-finite values.
Results may differ from a plain program's by a relative error of at most 0.008.
Values may be sent and summed in bfloat16 or wider, within the bound.
A program may use at most 64 MiB of HBM per device.

v0:
```python
import functools

import jax
import jax.numpy as jnp
from jax import lax
from jax.experimental import pallas as pl
from jax.experimental.pallas import tpu as pltpu
from jax.sharding import PartitionSpec as P

epsilon = 1e-06
F32 = jnp.float32
BF16 = jnp.bfloat16
MESH = pl.DeviceIdType.MESH


def tile_of(width, most):
    tile = most
    while width % tile:
        tile //= 2
    return tile


def dot(a, b):
    return lax.dot_general(a, b, (((1,), (0,)), ((), ())), preferred_element_type=F32)


def dot_t(a, b):
    return lax.dot_general(a, b, (((1,), (1,)), ((), ())), preferred_element_type=F32)


def placing(ids_row, own, experts, capacity, padded):
    count = ids_row.shape[1]
    down = lax.broadcasted_iota(jnp.int32, (count, count), 0)
    across = lax.broadcasted_iota(jnp.int32, (count, count), 1)
    rel = ids_row - own
    rel = jnp.where(rel < 0, rel + experts, rel).astype(F32)
    spread = jnp.broadcast_to(rel, (count, count))
    column = jnp.sum(jnp.where(down == across, spread, 0.0), axis=1, keepdims=True)
    before = jnp.where((column == spread) & (down < across), 1.0, 0.0)
    rank = jnp.sum(before, axis=0, keepdims=True)
    slot = jnp.broadcast_to(rel * capacity + rank, (count, count))
    slot_column = jnp.sum(jnp.where(down == across, slot, 0.0), axis=1, keepdims=True)
    gather = jnp.where(down.astype(F32) == slot, 1.0, 0.0)
    wide = lax.broadcasted_iota(jnp.int32, (count, padded), 1).astype(F32)
    scatter = jnp.where(slot_column == wide, 1.0, 0.0).astype(BF16)
    return gather, scatter


def kernel(
    dims,
    fid_hbm, fgate_hbm, gid_hbm, ggate_hbm, gain_hbm,
    x_hbm, g_hbm, saved_hbm, acts_hbm, wi_hbm, wo_hbm,
    fin_f, fin_b, ur_f, ur_b,
    fid_ref, fgate_ref, gid_ref, ggate_ref, gain_ref,
    x_ref, g_ref, saved_ref, acts_ref, wi, wo, gain_f,
    xs_f, xs_b, rx_f, rx_b, gs_f, rg_f, us_f, us_b,
    part_f, part_b, rpart_f, rpart_b, own_f, own_b,
    mv, pb, ret_b, th, srt, hidden_ref, joined,
    w_sem,
    disp_s, disp_r, gate_s, gate_r, relay_s, relay_r, perm_s, perm_r, red_s, red_r,
    move_s, move_r, out_s, out_r, ret_s, ret_r,
):
    pipes, E, G = dims
    s = lax.axis_index("pipe")
    position = lax.axis_index("expert")
    e = position // G
    g = position % G
    C, D = xs_f.shape[1:]
    T = x_ref.shape[0]
    F = wo.shape[0]

    def dev(hop, k, j):
        return (
            (s + hop + pipes) % pipes,
            ((e + k + E) % E) * G + (g + j + G) % G,
        )

    peers = [dev(0, k, 0) for k in range(1, E)] + [dev(0, 0, j) for j in range(1, G)]
    peers += [dev(hop, k, 0) for hop in (1, -1) for k in range(E)]
    barrier = pltpu.get_barrier_semaphore()
    for peer in peers:
        pl.semaphore_signal(barrier, inc=1, device_id=peer, device_id_type=MESH)
    pairs = (
        (gid_hbm, gid_ref), (g_hbm, g_ref), (fid_hbm, fid_ref), (fgate_hbm, fgate_ref),
        (ggate_hbm, ggate_ref), (gain_hbm, gain_ref), (x_hbm, x_ref), (saved_hbm, saved_ref), (acts_hbm, acts_ref),
        (wo_hbm, wo), (wi_hbm, wi),
    )
    loads = [
        pltpu.make_async_copy(source, held, w_sem.at[i]) for i, (source, held) in enumerate(pairs)
    ]
    for load in loads:
        load.start()
    load_gid, load_g, *load_small, load_x, load_saved, load_acts, load_wo, load_wi = loads

    started = []

    def remote(src, dst, send, recv, target):
        copy = pltpu.make_async_remote_copy(
            src_ref=src, dst_ref=dst, send_sem=send, recv_sem=recv,
            device_id=target, device_id_type=MESH,
        )
        copy.start()
        started.append(copy)
        return copy

    xs, rx = (xs_f, xs_b), (rx_f, rx_b)
    part, rpart = (part_f, part_b), (rpart_f, rpart_b)
    own = (own_f, own_b)
    halves = 2 if C % 32 == 0 else 1
    half = C // halves

    load_gid.wait()
    gather_b, scatter_b = placing(gid_ref[...], e, E, C, us_b.shape[1])
    gather_b_rows = gather_b.astype(BF16)
    load_g.wait()
    xs_b[...] = dot(gather_b_rows, g_ref[...]).reshape(E, C, D).astype(BF16)

    pl.semaphore_wait(barrier, len(peers))

    disp, gate_copy, relay = {}, {}, {}
    for k in range(1, E):
        disp[1, k] = remote(
            xs_b.at[k], rx_b.at[k, 0], disp_s.at[1, k], disp_r.at[1, k], dev(0, k, 0)
        )
    for j in range(1, G):
        relay[1, 0, j] = remote(
            xs_b.at[0], rx_b.at[0, j], relay_s.at[1, 0, j], relay_r.at[1, 0, j], dev(0, 0, j)
        )
    for load in load_small:
        load.wait()
    gather_f, scatter_f = placing(fid_ref[...], e, E, C, us_f.shape[1])
    load_x.wait()
    xs_f[...] = dot(gather_f.astype(BF16), x_ref[...]).reshape(E, C, D).astype(BF16)
    for k in range(E):
        disp[0, k] = remote(
            xs_f.at[k], rx_f.at[k, 0], disp_s.at[0, k], disp_r.at[0, k], dev(1, k, 0)
        )
    us_b[...] = scatter_b
    us_f[...] = scatter_f
    gates_b = jnp.sum(gather_b * ggate_ref[...], axis=1, keepdims=True)
    gates_f = jnp.sum(gather_f * fgate_ref[...], axis=1, keepdims=True)
    gs_f[...] = jnp.broadcast_to(gates_f, (T, gs_f.shape[2])).reshape(gs_f.shape)
    gain_copy = remote(gain_ref, gain_f, perm_s.at[2], perm_r.at[2], dev(1, 0, 0))
    for k in range(E):
        gate_copy[k] = remote(gs_f.at[k], rg_f.at[k], gate_s.at[k], gate_r.at[k], dev(1, k, 0))
    perm = (
        remote(us_f, ur_f, perm_s.at[0], perm_r.at[0], dev(1, 0, 0)),
        remote(us_b, ur_b, perm_s.at[1], perm_r.at[1], dev(-1, 0, 0)),
    )

    rx_b[0, 0] = xs_b[0]
    load_saved.wait()
    srt[...] = dot(gather_b_rows, saved_ref[...]).reshape(E, C, D).astype(BF16)

    def pass_on(b, k):
        disp[b, k].wait_recv()
        for j in range(1, G):
            relay[b, k, j] = remote(
                rx[b].at[k, 0], rx[b].at[k, j], relay_s.at[b, k, j], relay_r.at[b, k, j],
                dev(0, 0, j),
            )

    def arrived(b, k):
        for j in range(1, G):
            relay[b, k, j].wait_recv()

    tile_f = tile_of(F, 256)
    tile_d = tile_of(D, 512)
    reduce = {}

    def put_part(b, k, rows, columns):
        rows = rows.reshape(G, C, tile_d)
        own[b][k, :, columns] = rows[0]
        for j in range(1, G):
            part[b][k, j, :, columns] = rows[G - j].astype(BF16)

    def send_part(b, k):
        for j in range(1, G):
            reduce[b, k, j] = remote(
                part[b].at[k, j], rpart[b].at[k, j], red_s.at[b, k, j], red_r.at[b, k, j],
                dev(0, 0, j),
            )

    def summed(b, k):
        total = own[b][k]
        for j in range(1, G):
            reduce[b, k, j].wait_recv()
            total = total + rpart[b][k, j].astype(F32)
        return total

    def forward_first():
        for k in range(E):
            arrived(0, k)
        rows = rx_f[...].astype(F32).reshape(E * G * C, D)
        inverse = lax.rsqrt(jnp.mean(rows * rows, axis=-1, keepdims=True) + epsilon)
        normed = (rows * inverse * gain_f[...]).astype(BF16)
        for f in range(0, F, tile_f):
            gate = dot(normed, wi[:, f : f + tile_f])
            up = dot(normed, wi[:, F + f : F + f + tile_f])
            hidden_ref[:, f : f + tile_f] = (jax.nn.silu(gate) * up).astype(BF16)

    def forward_second():
        hidden = hidden_ref[...]

        def step(i, carry):
            columns = pl.ds(pl.multiple_of(i * tile_d, tile_d), tile_d)
            rows = dot(hidden, wo[:, columns]).reshape(E, G, C, tile_d)
            for k in range(E):
                put_part(0, k, rows[k], columns)
            return carry

        lax.fori_loop(0, D // tile_d, step, 0)
        for k in reversed(range(E)):
            send_part(0, k)

    def forward_end(k):
        total = summed(0, k)
        gate_copy[k].wait_recv()
        moved = (rx_f[k, 0].astype(F32) + rg_f[k][:, :1] * total).astype(BF16)
        if k == 0:
            mv[0] = moved
            own_move = pltpu.make_async_copy(mv.at[0], fin_f.at[0], move_s.at[0])
            own_move.start()
            own_moves.append(own_move)
            return
        mv[k] = moved
        ends.append(
            remote(mv.at[k], fin_f.at[k], move_s.at[k], move_r.at[k], dev(0, -k, 0))
        )

    def backward_first(k):
        arrived(1, k)
        rows = rx_b[k].astype(F32).reshape(G * C, D).astype(BF16)
        acts = []
        for j in range(G):
            source = ((e - k + E) % E) * G + (g - j + G) % G
            acts.append(acts_ref[source].astype(F32))
        acts = jnp.concatenate(acts, axis=0)
        for f in range(0, F, tile_f):
            grad = dot_t(rows, wo[f : f + tile_f, :])
            gate_act = acts[:, f : f + tile_f]
            up_act = acts[:, F + f : F + f + tile_f]
            squashed = jax.nn.sigmoid(gate_act)
            joined[:, f : f + tile_f] = (
                grad * up_act * squashed * (1.0 + gate_act * (1.0 - squashed))
            ).astype(BF16)
            joined[:, F + f : F + f + tile_f] = (grad * gate_act * squashed).astype(BF16)

    def backward_second(k):
        both = joined[...]

        def step(i, carry):
            columns = pl.ds(pl.multiple_of(i * tile_d, tile_d), tile_d)
            put_part(1, k, dot_t(both, wi[columns, :]), columns)
            return carry

        lax.fori_loop(0, D // tile_d, step, 0)
        send_part(1, k)

    back = {}

    def backward_return(k):
        pb[k] = summed(1, k).astype(BF16)
        for h in range(halves):
            rows = pl.ds(h * half, half)
            back[k, h] = remote(
                pb.at[k, rows], ret_b.at[k, rows], ret_s.at[k, h], ret_r.at[k, h], dev(0, -k, 0)
            )

    def backward_end(k, h):
        low, high = h * half, (h + 1) * half
        if k:
            back[k, h].wait_recv()
            pulled = ret_b[k, low:high].astype(F32)
        else:
            pulled = own_b[0, low:high]
            for j in range(1, G):
                if h == 0:
                    reduce[1, 0, j].wait_recv()
                pulled = pulled + rpart_b[0, j, low:high].astype(F32)
        weighted = gates_b[k * C + low : k * C + high] * pulled * gain_ref[...]
        before = srt[k, low:high].astype(F32)
        inverse = lax.rsqrt(jnp.mean(before * before, axis=-1, keepdims=True) + epsilon)
        unit = before * inverse
        inner = jnp.mean(weighted * unit, axis=-1, keepdims=True)
        th[k, low:high] = (
            xs_b[k, low:high].astype(F32) + inverse * (weighted - unit * inner)
        ).astype(BF16)
        rows = pl.ds(low, half)
        ends.append(
            remote(
                th.at[k, rows], fin_b.at[k, rows], out_s.at[k, h], out_r.at[k, h], dev(-1, 0, 0)
            )
        )

    ends = []
    own_moves = []
    load_wo.wait()
    load_acts.wait()
    backward_first(0)
    load_wi.wait()
    backward_second(0)
    for k in range(1, E):
        pass_on(1, k)
    for h in range(halves):
        backward_end(0, h)
    for k in range(1, E):
        backward_first(k)
        backward_second(k)
    for k in range(E):
        pass_on(0, k)
    for k in range(1, E):
        backward_return(k)
    gain_copy.wait_recv()
    forward_first()
    forward_second()
    for k in range(1, E):
        forward_end(k)
    for k in range(1, E):
        for h in range(halves):
            backward_end(k, h)
    forward_end(0)

    perm[0].wait_recv()
    perm[1].wait_recv()
    for copy in ends:
        copy.wait_recv()
    for copy in own_moves:
        copy.wait()
    for copy in started:
        copy.wait_send()


def unsort(fin_f, fin_b, ur_f, ur_b, fout_ref, gout_ref):
    T, width = fout_ref.shape
    for fin, ur, out in ((fin_f, ur_f, fout_ref), (fin_b, ur_b, gout_ref)):
        rows = fin[...].astype(F32).reshape(T, width).astype(BF16)
        out[...] = dot(ur[:, :T], rows).astype(BF16)


def on_device(
    dims,
    forward_in,
    forward_ids,
    forward_gates,
    grad_in,
    grad_ids,
    grad_gates,
    saved_input,
    saved_acts,
    norm_gain,
    weight_in,
    weight_out,
):
    pipes, E, G = dims
    T, D = forward_in.shape[1:]
    F = weight_out.shape[1]
    C = T // E
    padded = -(-T // 128) * 128
    DMA = pltpu.SemaphoreType.DMA
    rows = (E, C, D)
    vmem = pl.BlockSpec(memory_space=pltpu.VMEM)
    hbm = pl.BlockSpec(memory_space=pl.ANY)
    sorted_rows = jax.ShapeDtypeStruct(rows, BF16)
    order = jax.ShapeDtypeStruct((T, padded), BF16)
    halves = 2 if C % 32 == 0 else 1
    arrived = pl.pallas_call(
        functools.partial(kernel, dims),
        out_shape=(sorted_rows, sorted_rows, order, order),
        in_specs=[hbm] * 11,
        out_specs=(hbm, hbm, vmem, vmem),
        scratch_shapes=[
            pltpu.VMEM((1, T), jnp.int32), pltpu.VMEM((1, T), F32),
            pltpu.VMEM((1, T), jnp.int32), pltpu.VMEM((1, T), F32),
            pltpu.VMEM((1, D), F32),
            pltpu.VMEM((T, D), BF16), pltpu.VMEM((T, D), BF16), pltpu.VMEM((T, D), BF16),
            pltpu.VMEM((E * G, C, 2 * F), BF16),
            pltpu.VMEM((D, 2 * F), BF16),
            pltpu.VMEM((F, D), BF16),
            pltpu.VMEM((1, D), F32),
            pltpu.VMEM(rows, BF16), pltpu.VMEM(rows, BF16),
            pltpu.VMEM((E, G, C, D), BF16), pltpu.VMEM((E, G, C, D), BF16),
            pltpu.VMEM((E, C, 128), F32), pltpu.VMEM((E, C, 128), F32),
            pltpu.VMEM((T, padded), BF16), pltpu.VMEM((T, padded), BF16),
            pltpu.VMEM((E, G, C, D), BF16), pltpu.VMEM((E, G, C, D), BF16),
            pltpu.VMEM((E, G, C, D), BF16), pltpu.VMEM((E, G, C, D), BF16),
            pltpu.VMEM(rows, F32), pltpu.VMEM(rows, F32),
            pltpu.VMEM(rows, BF16), pltpu.VMEM(rows, BF16), pltpu.VMEM(rows, BF16),
            pltpu.VMEM(rows, BF16), pltpu.VMEM(rows, BF16),
            pltpu.VMEM((E * G * C, F), BF16),
            pltpu.VMEM((G * C, 2 * F), BF16),
            DMA((11,)),
            DMA((2, E)), DMA((2, E)), DMA((E,)), DMA((E,)),
            DMA((2, E, G)), DMA((2, E, G)), DMA((3,)), DMA((3,)),
            DMA((2, E, G)), DMA((2, E, G)), DMA((E,)), DMA((E,)),
            DMA((E, halves)), DMA((E, halves)), DMA((E, halves)), DMA((E, halves)),
        ],
        compiler_params=pltpu.CompilerParams(
            collective_id=0, has_side_effects=True, vmem_limit_bytes=60 * 2**20
        ),
    )(
        forward_ids.reshape(1, T),
        forward_gates.reshape(1, T),
        grad_ids.reshape(1, T),
        grad_gates.reshape(1, T),
        norm_gain,
        forward_in[0],
        grad_in[0],
        saved_input[0],
        saved_acts.reshape(E * G, C, 2 * F),
        weight_in[0],
        weight_out[0],
    )
    width = D // 2
    wide = pl.BlockSpec((E, C, width), lambda i: (0, 0, i))
    whole = pl.BlockSpec((T, padded), lambda i: (0, 0))
    out = pl.BlockSpec((T, width), lambda i: (0, i))
    out_shape = jax.ShapeDtypeStruct((T, D), BF16)
    fwd, grad = pl.pallas_call(
        unsort,
        grid=(2,),
        out_shape=(out_shape, out_shape),
        in_specs=[wide, wide, whole, whole],
        out_specs=(out, out),
    )(*arrived)
    return fwd[None], grad[None]


def solution(mesh):
    sources = mesh.shape["expert"]
    G = min(4, sources // 2)
    dims = (mesh.shape["pipe"], sources // G, G)
    placed = (
        P("pipe", "expert", None),
        P("pipe", "expert", None),
        P("pipe", "expert", None),
        P("pipe", "expert", None),
        P("pipe", "expert", None),
        P("pipe", "expert", None),
        P("pipe", "expert", None),
        P("pipe", "expert", None, None),
        P("pipe", None),
        P("expert", None, None),
        P("expert", None, None),
    )
    return jax.shard_map(
        functools.partial(on_device, dims),
        mesh=mesh,
        in_specs=placed,
        out_specs=(P("pipe", "expert", None), P("pipe", "expert", None)),
        check_vma=False,
    )
```

profile of v0, /device:TPU:0, one launch (start us, length us, event | category | flops | bytes accessed | tf_op | source)
XLA Modules:
  0.0 40.6 jit_solution(2504128961905915110)
XLA Ops:
  0.6 37.7 %shard_map.122 = (bf16[2,32,3584]{2,1,0:T(8,128)(2,1)}, bf16[2,32,3584]{2,1,0:T(8,128)(2,1)}, bf16[64,128]{1,0:T(8,128)(2,1)}, bf16[64,128]{1,0:T(8,128)(2,1)}) custom-call(s32[1,64]{1,0:T(1,128)} %bitcast.18, f32[1,64]{1,0:T(1,128)} %bitcast.19, s32[1,64]{1,0:T(1,128)} %bitcast.20, f32[1,64]{1,0:T(1,128)} %bitcast.21, f32[1,3584]{1,0:T(1,128)} %gain_hbm.1, ...), custom_call_target="tpu_custom_call" | custom-call | tf_op jit(solution)/shard_map/pallas_call | solution.py:367
  38.3 2.3 %shard_map.123 = (bf16[64,3584]{1,0:T(8,128)(2,1)}, bf16[64,3584]{1,0:T(8,128)(2,1)}) custom-call(bf16[2,32,3584]{2,1,0:T(8,128)(2,1)} %get-tuple-element.8.fin_f, bf16[2,32,3584]{2,1,0:T(8,128)(2,1)} %get-tuple-element.9.fin_b, bf16[64,128]{1,0:T(8,128)(2,1)} %get-tuple-element.10.ur_f, bf16[64,128]{1,0:T(8,128)(2,1)} %get-tuple-element.11.ur_b), custom_call_target="tpu_custom_call" | custom-call | tf_op jit(solution)/shard_map/pallas_call | solution.py:419
where the time goes:
time: 40.8 us; the launch traced here: 40.6 us
  Pallas kernels  40 us (98%)
  between operations  0.64 us (2%)
    pallas_call x1, Pallas kernels, on_device(): pl.pallas_call(functools.partial(kernel, dims), out_shape=(sorted_rows, s...  37.7 us
    pallas_call x1, Pallas kernels, on_device(): pl.pallas_call(unsort, grid=(2,), out_shape=(out_shape, out_shape), in_sp...  2.32 us

commit v1 on v0

--- a/solution.py
+++ b/solution.py
@@ -56,7 +56,7 @@
     xs_f, xs_b, rx_f, rx_b, gs_f, rg_f, us_f, us_b,
     part_f, part_b, rpart_f, rpart_b, own_f, own_b,
     mv, pb, ret_b, th, srt, hidden_ref, joined,
-    w_sem,
+    w_sem, ready_sem,
     disp_s, disp_r, gate_s, gate_r, relay_s, relay_r, perm_s, perm_r, red_s, red_r,
     move_s, move_r, out_s, out_r, ret_s, ret_r,
 ):
@@ -75,11 +75,19 @@
             ((e + k + E) % E) * G + (g + j + G) % G,
         )
 
-    peers = [dev(0, k, 0) for k in range(1, E)] + [dev(0, 0, j) for j in range(1, G)]
-    peers += [dev(hop, k, 0) for hop in (1, -1) for k in range(E)]
+    near = [dev(0, k, 0) for k in range(1, E)] + [dev(0, 0, j) for j in range(1, G)]
+    following = [dev(1, k, 0) for k in range(E)]
+    previous = [dev(-1, k, 0) for k in range(E)]
+    first, last = s == 0, s == pipes - 1
+
+    def greet(sem, peers):
+        for peer in peers:
+            pl.semaphore_signal(sem, inc=1, device_id=peer, device_id_type=MESH)
+
     barrier = pltpu.get_barrier_semaphore()
-    for peer in peers:
-        pl.semaphore_signal(barrier, inc=1, device_id=peer, device_id_type=MESH)
+    greet(barrier, near)
+    greet(barrier, previous)
+    pl.when(s != pipes - 1)(lambda: greet(barrier, following))
     pairs = (
         (gid_hbm, gid_ref), (g_hbm, g_ref), (fid_hbm, fid_ref), (fgate_hbm, fgate_ref),
         (ggate_hbm, ggate_ref), (gain_hbm, gain_ref), (x_hbm, x_ref), (saved_hbm, saved_ref), (acts_hbm, acts_ref),
@@ -109,13 +117,17 @@
     halves = 2 if C % 32 == 0 else 1
     half = C // halves
 
-    load_gid.wait()
+    with jax.named_scope("w_gid"):
+        load_gid.wait()
     gather_b, scatter_b = placing(gid_ref[...], e, E, C, us_b.shape[1])
     gather_b_rows = gather_b.astype(BF16)
-    load_g.wait()
+    with jax.named_scope("w_bar"):
+        pl.semaphore_wait(barrier, len(near) + E * (1 + (s + pipes - 1) // pipes))
+    pl.when(last)(lambda: greet(ready_sem, following))
+    with jax.named_scope("w_g"):
+        load_g.wait()
     xs_b[...] = dot(gather_b_rows, g_ref[...]).reshape(E, C, D).astype(BF16)
 
-    pl.semaphore_wait(barrier, len(peers))
 
     disp, gate_copy, relay = {}, {}, {}
     for k in range(1, E):
@@ -129,7 +141,8 @@
     for load in load_small:
         load.wait()
     gather_f, scatter_f = placing(fid_ref[...], e, E, C, us_f.shape[1])
-    load_x.wait()
+    with jax.named_scope("w_x"):
+        load_x.wait()
     xs_f[...] = dot(gather_f.astype(BF16), x_ref[...]).reshape(E, C, D).astype(BF16)
     for k in range(E):
         disp[0, k] = remote(
@@ -143,13 +156,11 @@
     gain_copy = remote(gain_ref, gain_f, perm_s.at[2], perm_r.at[2], dev(1, 0, 0))
     for k in range(E):
         gate_copy[k] = remote(gs_f.at[k], rg_f.at[k], gate_s.at[k], gate_r.at[k], dev(1, k, 0))
-    perm = (
-        remote(us_f, ur_f, perm_s.at[0], perm_r.at[0], dev(1, 0, 0)),
-        remote(us_b, ur_b, perm_s.at[1], perm_r.at[1], dev(-1, 0, 0)),
-    )
+    perm_f = remote(us_f, ur_f, perm_s.at[0], perm_r.at[0], dev(1, 0, 0))
 
     rx_b[0, 0] = xs_b[0]
-    load_saved.wait()
+    with jax.named_scope("w_saved"):
+        load_saved.wait()
     srt[...] = dot(gather_b_rows, saved_ref[...]).reshape(E, C, D).astype(BF16)
 
     def pass_on(b, k):
@@ -202,14 +213,11 @@
     def forward_second():
         hidden = hidden_ref[...]
 
-        def step(i, carry):
-            columns = pl.ds(pl.multiple_of(i * tile_d, tile_d), tile_d)
+        for d in range(0, D, tile_d):
+            columns = slice(d, d + tile_d)
             rows = dot(hidden, wo[:, columns]).reshape(E, G, C, tile_d)
             for k in range(E):
                 put_part(0, k, rows[k], columns)
-            return carry
-
-        lax.fori_loop(0, D // tile_d, step, 0)
         for k in reversed(range(E)):
             send_part(0, k)
 
@@ -218,10 +226,7 @@
         gate_copy[k].wait_recv()
         moved = (rx_f[k, 0].astype(F32) + rg_f[k][:, :1] * total).astype(BF16)
         if k == 0:
-            mv[0] = moved
-            own_move = pltpu.make_async_copy(mv.at[0], fin_f.at[0], move_s.at[0])
-            own_move.start()
-            own_moves.append(own_move)
+            fin_f[0] = moved
             return
         mv[k] = moved
         ends.append(
@@ -249,12 +254,9 @@
     def backward_second(k):
         both = joined[...]
 
-        def step(i, carry):
-            columns = pl.ds(pl.multiple_of(i * tile_d, tile_d), tile_d)
+        for d in range(0, D, tile_d):
+            columns = slice(d, d + tile_d)
             put_part(1, k, dot_t(both, wi[columns, :]), columns)
-            return carry
-
-        lax.fori_loop(0, D // tile_d, step, 0)
         send_part(1, k)
 
     back = {}
@@ -294,48 +296,80 @@
         )
 
     ends = []
-    own_moves = []
-    load_wo.wait()
+    with jax.named_scope("w_wo"):
+        load_wo.wait()
     load_acts.wait()
-    backward_first(0)
-    load_wi.wait()
-    backward_second(0)
-    for k in range(1, E):
-        pass_on(1, k)
+    with jax.named_scope("b1_0"):
+        backward_first(0)
+    with jax.named_scope("w_wi"):
+        load_wi.wait()
+    with jax.named_scope("b2_0"):
+        backward_second(0)
+    for k in range(1, E):
+        with jax.named_scope("pass1"):
+            pass_on(1, k)
+    with jax.named_scope("w_prev"):
+        pl.when(first)(lambda: pl.semaphore_wait(ready_sem, E))
+    perm_b = remote(us_b, ur_b, perm_s.at[1], perm_r.at[1], dev(-1, 0, 0))
     for h in range(halves):
-        backward_end(0, h)
-    for k in range(1, E):
-        backward_first(k)
-        backward_second(k)
+        with jax.named_scope("bend0"):
+            backward_end(0, h)
+    for k in range(1, E):
+        with jax.named_scope("b1_1"):
+            backward_first(k)
+        with jax.named_scope("b2_1"):
+            backward_second(k)
+    for k in range(1, E):
+        with jax.named_scope("bret"):
+            backward_return(k)
     for k in range(E):
-        pass_on(0, k)
-    for k in range(1, E):
-        backward_return(k)
-    gain_copy.wait_recv()
-    forward_first()
-    forward_second()
-    for k in range(1, E):
-        forward_end(k)
+        with jax.named_scope("pass0"):
+            pass_on(0, k)
+    with jax.named_scope("w_gain"):
+        gain_copy.wait_recv()
+    with jax.named_scope("f1"):
+        forward_first()
+    with jax.named_scope("f2"):
+        forward_second()
+    for k in range(1, E):
+        with jax.named_scope("fend1"):
+            forward_end(k)
     for k in range(1, E):
         for h in range(halves):
-            backward_end(k, h)
-    forward_end(0)
-
-    perm[0].wait_recv()
-    perm[1].wait_recv()
+            with jax.named_scope("bend1"):
+                backward_end(k, h)
+    with jax.named_scope("fend0"):
+        forward_end(0)
+
+    with jax.named_scope("w_perm0"):
+        perm_f.wait_recv()
+    with jax.named_scope("w_perm1"):
+        perm_b.wait_recv()
     for copy in ends:
-        copy.wait_recv()
-    for copy in own_moves:
+        with jax.named_scope("w_end"):
+            copy.wait_recv()
+    with jax.named_scope("w_sends"):
+        for copy in started:
+            copy.wait_send()
+
+
+UNSORT_STEPS = 2
+
+
+def unsort(fin_f, fin_b, ur_f, ur_b, fout_hbm, gout_hbm, held, sems):
+    T, D = fout_hbm.shape
+    width = D // UNSORT_STEPS
+    copies = []
+    for i, (fin, ur, out) in enumerate(((fin_f, ur_f, fout_hbm), (fin_b, ur_b, gout_hbm))):
+        for c in range(UNSORT_STEPS):
+            columns = pl.ds(c * width, width)
+            rows = fin[:, :, columns].astype(F32).reshape(T, width).astype(BF16)
+            held[i, :, columns] = dot(ur[:, :T], rows).astype(BF16)
+            copy = pltpu.make_async_copy(held.at[i, :, columns], out.at[:, columns], sems.at[i, c])
+            copy.start()
+            copies.append(copy)
+    for copy in copies:
         copy.wait()
-    for copy in started:
-        copy.wait_send()
-
-
-def unsort(fin_f, fin_b, ur_f, ur_b, fout_ref, gout_ref):
-    T, width = fout_ref.shape
-    for fin, ur, out in ((fin_f, ur_f, fout_ref), (fin_b, ur_b, gout_ref)):
-        rows = fin[...].astype(F32).reshape(T, width).astype(BF16)
-        out[...] = dot(ur[:, :T], rows).astype(BF16)
 
 
 def on_device(
@@ -366,9 +400,9 @@
     halves = 2 if C % 32 == 0 else 1
     arrived = pl.pallas_call(
         functools.partial(kernel, dims),
-        out_shape=(sorted_rows, sorted_rows, order, order),
+        out_shape=(pltpu.VMEM(rows, BF16), pltpu.VMEM(rows, BF16), pltpu.VMEM((T, padded), BF16), pltpu.VMEM((T, padded), BF16)),
         in_specs=[hbm] * 11,
-        out_specs=(hbm, hbm, vmem, vmem),
+        out_specs=(vmem, vmem, vmem, vmem),
         scratch_shapes=[
             pltpu.VMEM((1, T), jnp.int32), pltpu.VMEM((1, T), F32),
             pltpu.VMEM((1, T), jnp.int32), pltpu.VMEM((1, T), F32),
@@ -389,40 +423,40 @@
             pltpu.VMEM(rows, BF16), pltpu.VMEM(rows, BF16),
             pltpu.VMEM((E * G * C, F), BF16),
             pltpu.VMEM((G * C, 2 * F), BF16),
-            DMA((11,)),
+            DMA((11,)), pltpu.SemaphoreType.REGULAR,
             DMA((2, E)), DMA((2, E)), DMA((E,)), DMA((E,)),
             DMA((2, E, G)), DMA((2, E, G)), DMA((3,)), DMA((3,)),
             DMA((2, E, G)), DMA((2, E, G)), DMA((E,)), DMA((E,)),
             DMA((E, halves)), DMA((E, halves)), DMA((E, halves)), DMA((E, halves)),
         ],
         compiler_params=pltpu.CompilerParams(
-            collective_id=0, has_side_effects=True, vmem_limit_bytes=60 * 2**20
+            collective_id=0, has_side_effects=True, vmem_limit_bytes=40 * 2**20
         ),
-    )(
-        forward_ids.reshape(1, T),
-        forward_gates.reshape(1, T),
-        grad_ids.reshape(1, T),
-        grad_gates.reshape(1, T),
-        norm_gain,
-        forward_in[0],
-        grad_in[0],
-        saved_input[0],
-        saved_acts.reshape(E * G, C, 2 * F),
-        weight_in[0],
-        weight_out[0],
-    )
-    width = D // 2
-    wide = pl.BlockSpec((E, C, width), lambda i: (0, 0, i))
-    whole = pl.BlockSpec((T, padded), lambda i: (0, 0))
-    out = pl.BlockSpec((T, width), lambda i: (0, i))
+    )(*[
+        pltpu.with_memory_space_constraint(a, pltpu.HBM)
+        for a in (
+            forward_ids.reshape(1, T),
+            forward_gates.reshape(1, T),
+            grad_ids.reshape(1, T),
+            grad_gates.reshape(1, T),
+            norm_gain,
+            forward_in[0],
+            grad_in[0],
+            saved_input[0],
+            saved_acts.reshape(E * G, C, 2 * F),
+            weight_in[0],
+            weight_out[0],
+        )
+    ])
     out_shape = jax.ShapeDtypeStruct((T, D), BF16)
     fwd, grad = pl.pallas_call(
         unsort,
-        grid=(2,),
         out_shape=(out_shape, out_shape),
-        in_specs=[wide, wide, whole, whole],
-        out_specs=(out, out),
-    )(*arrived)
+        in_specs=[vmem] * 4,
+        out_specs=(hbm, hbm),
+        scratch_shapes=[pltpu.VMEM((2, T, D), BF16), DMA((2, UNSORT_STEPS))],
+        compiler_params=pltpu.CompilerParams(vmem_limit_bytes=8 * 2**20),
+    )(*[pltpu.with_memory_space_constraint(a, pltpu.VMEM) for a in arrived])
     return fwd[None], grad[None]
 
 

time: 40.8 us -> 35.4 us (0.87)
  Pallas kernels: 40 us -> 34.6 us
    pallas_call x2, Pallas kernels: 40 us -> 34.6 us  [the longest x1 33.5 us: on_device(): pl.pallas_call(functools.partial(kernel, dims), out_shape=(pltpu.VMEM(row...]
where the time goes in v1:
time: 35.4 us; the launch traced here: 35.3 us
  Pallas kernels  34.6 us (98%)
  between operations  0.64 us (2%)
    pallas_call x1, Pallas kernels, on_device(): pl.pallas_call(functools.partial(kernel, dims), out_shape=(pltpu.VMEM(row...  33.5 us
    pallas_call x1, Pallas kernels, on_device(): pl.pallas_call(unsort, out_shape=(out_shape, out_shape), in_specs=[vmem]...  1.17 us

profile of v1, /device:TPU:0, one launch (start us, length us, event | category | flops | bytes accessed | tf_op | source)
XLA Modules:
  0.0 35.3 jit_solution(15804358468949419985)
XLA Ops:
  0.6 33.5 %shard_map.122 = (bf16[2,32,3584]{2,1,0:T(8,128)(2,1)S(1)}, bf16[2,32,3584]{2,1,0:T(8,128)(2,1)S(1)}, bf16[64,128]{1,0:T(8,128)(2,1)S(1)}, bf16[64,128]{1,0:T(8,128)(2,1)S(1)}) custom-call(s32[1,64]{1,0:T(1,128)} %bitcast.18, f32[1,64]{1,0:T(1,128)} %bitcast.19, s32[1,64]{1,0:T(1,128)} %bitcast.20, f32[1,64]{1,0:T(1,128)} %bitcast.21, f32[1,3584]{1,0:T(1,128)} %gain_hbm.1, ...), custom_call_target="tpu_custom_call" | custom-call | tf_op jit(solution)/shard_map/pallas_call | solution.py:401
  34.1 1.2 %shard_map.123 = (bf16[64,3584]{1,0:T(8,128)(2,1)}, bf16[64,3584]{1,0:T(8,128)(2,1)}) custom-call(bf16[2,32,3584]{2,1,0:T(8,128)(2,1)S(1)} %get-tuple-element.8.fin_f, bf16[2,32,3584]{2,1,0:T(8,128)(2,1)S(1)} %get-tuple-element.9.fin_b, bf16[64,128]{1,0:T(8,128)(2,1)S(1)} %get-tuple-element.10.ur_f, bf16[64,128]{1,0:T(8,128)(2,1)S(1)} %get-tuple-element.11.ur_b), custom_call_target="tpu_custom_call" | custom-call | tf_op jit(solution)/shard_map/pallas_call | solution.py:452

commit v2 on v1

v2 whole, which is shorter than its diff:
```python
import functools

import jax
import jax.numpy as jnp
from jax import lax
from jax.experimental import pallas as pl
from jax.experimental.pallas import tpu as pltpu
from jax.sharding import PartitionSpec as P

epsilon = 1e-06
F32 = jnp.float32
BF16 = jnp.bfloat16
MESH = pl.DeviceIdType.MESH


def tile_of(width, most):
    tile = most
    while width % tile:
        tile //= 2
    return tile


LAG = 2


def disp_rows(C):
    return 2 if C % 32 == 0 else 1


def columns_of(D, C):
    tile = tile_of(D, 512)
    tiles = D // tile
    width = tile * (-(-tiles // 4) if C % 32 == 0 else tiles)
    return [slice(d, min(d + width, D)) for d in range(0, D, width)]


def dot(a, b):
    return lax.dot_general(a, b, (((1,), (0,)), ((), ())), preferred_element_type=F32)


def dot_t(a, b):
    return lax.dot_general(a, b, (((1,), (1,)), ((), ())), preferred_element_type=F32)


def placing(ids_row, own, experts, capacity, padded):
    count = ids_row.shape[1]
    down = lax.broadcasted_iota(jnp.int32, (count, count), 0)
    across = lax.broadcasted_iota(jnp.int32, (count, count), 1)
    rel = ids_row - own
    rel = jnp.where(rel < 0, rel + experts, rel).astype(F32)
    spread = jnp.broadcast_to(rel, (count, count))
    column = jnp.sum(jnp.where(down == across, spread, 0.0), axis=1, keepdims=True)
    before = jnp.where((column == spread) & (down < across), 1.0, 0.0)
    rank = jnp.sum(before, axis=0, keepdims=True)
    slot = jnp.broadcast_to(rel * capacity + rank, (count, count))
    slot_column = jnp.sum(jnp.where(down == across, slot, 0.0), axis=1, keepdims=True)
    gather = jnp.where(down.astype(F32) == slot, 1.0, 0.0)
    wide = lax.broadcasted_iota(jnp.int32, (count, padded), 1).astype(F32)
    scatter = jnp.where(slot_column == wide, 1.0, 0.0).astype(BF16)
    return gather, scatter


def kernel(
    dims,
    fid_hbm, fgate_hbm, gid_hbm, ggate_hbm, gain_hbm,
    x_hbm, g_hbm, saved_hbm, acts_hbm, wi_hbm, wo_hbm,
    fin_f, fin_b, ur_f, ur_b,
    fid_ref, fgate_ref, gid_ref, ggate_ref, gain_ref,
    x_ref, g_ref, saved_ref, acts_ref, wi, wo, gain_f,
    xs_f, xs_b, rx_f, rx_b, gs_f, rg_f, us_f, us_b,
    part_f, part_b, rpart_f, rpart_b, own_f, own_b,
    mv, pb, ret_b, th, srt, hidden_ref, joined, sum_b, both_b, sum_f, square_f,
    via, w_sem, ready_sem, via_s, via_r,
    disp_s, disp_r, gate_s, gate_r, relay_s, relay_r, perm_s, perm_r, red_s, red_r, near_r,
    move_s, move_r, out_s, out_r, ret_s, ret_r,
):
    pipes, E, G = dims
    s = lax.axis_index("pipe")
    position = lax.axis_index("expert")
    e = position // G
    g = position % G
    C, D = xs_f.shape[1:]
    T = x_ref.shape[0]
    F = wo.shape[0]

    def dev(hop, k, j):
        return (
            (s + hop + pipes) % pipes,
            ((e + k + E) % E) * G + (g + j + G) % G,
        )

    near = [dev(0, k, 0) for k in range(1, E)] + [dev(0, 0, j) for j in range(1, G)]
    following = [dev(1, k, 0) for k in range(E)]
    previous = [dev(-1, k, 0) for k in range(E)]
    first, last = s == 0, s == pipes - 1

    def greet(sem, peers):
        for peer in peers:
            pl.semaphore_signal(sem, inc=1, device_id=peer, device_id_type=MESH)

    barrier = pltpu.get_barrier_semaphore()
    greet(barrier, near)
    greet(barrier, previous)
    pl.when(s != pipes - 1)(lambda: greet(barrier, following))
    pairs = (
        (gid_hbm, gid_ref), (g_hbm, g_ref), (fid_hbm, fid_ref), (fgate_hbm, fgate_ref),
        (ggate_hbm, ggate_ref), (gain_hbm, gain_ref), (x_hbm, x_ref), (saved_hbm, saved_ref), (acts_hbm, acts_ref),
        (wo_hbm, wo), (wi_hbm, wi),
    )
    loads = [
        pltpu.make_async_copy(source, held, w_sem.at[i]) for i, (source, held) in enumerate(pairs)
    ]
    for load in loads:
        load.start()
    load_gid, load_g, *load_small, load_x, load_saved, load_acts, load_wo, load_wi = loads

    def remote(src, dst, send, recv, target):
        copy = pltpu.make_async_remote_copy(
            src_ref=src, dst_ref=dst, send_sem=send, recv_sem=recv,
            device_id=target, device_id_type=MESH,
        )
        copy.start()
        return copy

    def whole(src, dst, send, recv, target=None):
        return pltpu.make_async_remote_copy(
            src_ref=src, dst_ref=dst, send_sem=send, recv_sem=recv,
            device_id=dev(1, 0, 0) if target is None else target, device_id_type=MESH,
        )

    xs, rx = (xs_f, xs_b), (rx_f, rx_b)
    part, rpart = (part_f, part_b), (rpart_f, rpart_b)
    own = (own_f, own_b)
    halves = disp_rows(C)
    half = C // halves
    tile_d = tile_of(D, 512)
    chunks = columns_of(D, C)
    count = len(chunks)
    others = range(1, E)

    def flat(rows):
        if C % 16:
            return rows.astype(F32).reshape(-1, rows.shape[-1]).astype(BF16)
        return rows.reshape(-1, rows.shape[-1])

    relay, reduce = {}, {}

    def outgoing(b, k, c):
        return pltpu.make_async_remote_copy(
            src_ref=xs[b].at[k, :, chunks[c]], dst_ref=rx[b].at[k, 0, :, chunks[c]],
            send_sem=disp_s.at[b * (E - 1) + k], recv_sem=disp_r.at[b * (E - 1) + k, c],
            device_id=dev(1 - b, k, 0), device_id_type=MESH,
        )

    def share(b, k, c, source):
        for j in range(1, G):
            relay[b, k, j, c] = remote(
                source, rx[b].at[k, j, :, chunks[c]],
                relay_s.at[b, k, j - 1], relay_r.at[b, k, j - 1, c], dev(0, 0, j),
            )

    def pass_on(b, k, c):
        with jax.named_scope(f"pass_{b}_{k}_{c}"):
            outgoing(b, k, c).wait_recv()
            share(b, k, c, rx[b].at[k, 0, :, chunks[c]])

    def arrived(b, k, c):
        with jax.named_scope(f"arr_{b}_{k}_{c}"):
            for j in range(1, G):
                relay[b, k, j, c].wait_recv()

    def put_part(b, k, rows, columns):
        rows = rows.reshape(G, C, rows.shape[-1])
        own[b][k, :, columns] = rows[0]
        for j in range(1, G):
            part[b][k, j, :, columns] = rows[G - j].astype(BF16)

    def send_part(b, k, c):
        for j in range(1, G):
            reduce[b, k, j, c] = remote(
                part[b].at[k, j, :, chunks[c]], rpart[b].at[k, j, :, chunks[c]],
                red_s.at[b, k, j - 1], landed(b, k, j, c), dev(0, 0, j),
            )

    def landed(b, k, j, c):
        return red_r.at[b, k - 1, j - 1, c] if k else near_r.at[b, j - 1]

    def wait_near(b):
        for j in range(1, G):
            whole(
                part[b].at[0, j], rpart[b].at[0, j], red_s.at[b, 0, j - 1], near_r.at[b, j - 1]
            ).wait_recv()

    def summed(b, k, c):
        total = own[b][k, :, chunks[c]]
        for j in range(1, G):
            if k:
                with jax.named_scope(f"red_{b}_{k}_{c}"):
                    reduce[b, k, j, c].wait_recv()
            total = total + rpart[b][k, j, :, chunks[c]].astype(F32)
        return total

    def backward_first(k, c):
        arrived(1, k, c)
        grad = dot_t(flat(rx_b[k, :, :, chunks[c]]), wo[:, chunks[c]])
        sum_b[...] = grad if c == 0 else sum_b[...] + grad

    def backward_hidden(k):
        for j in range(G):
            source = ((e - k + E) % E) * G + (g - j + G) % G
            rows = slice(j * C, (j + 1) * C)
            grad = sum_b[rows, :]
            acts = acts_ref[source].astype(F32)
            gate_act, up_act = acts[:, :F], acts[:, F:]
            squashed = jax.nn.sigmoid(gate_act)
            gate_grad = grad * up_act * squashed * (1.0 + gate_act * (1.0 - squashed))
            both_b[rows, :F] = gate_grad
            both_b[rows, F:] = grad * gate_act * squashed
        joined[...] = both_b[...].astype(BF16)

    def backward_second(k, c):
        for d in range(chunks[c].start, chunks[c].stop, tile_d):
            columns = slice(d, d + tile_d)
            put_part(1, k, dot_t(joined[...], wi[columns, :]), columns)
        send_part(1, k, c)

    def send_back(k, c, h):
        rows = slice(h * half, (h + 1) * half)
        remote(
            pb.at[k, rows, chunks[c]], ret_b.at[k, rows, chunks[c]],
            ret_s.at[k - 1], ret_r.at[k - 1, h], dev(0, -k, 0),
        )

    def backward_return(k, c):
        pb[k, :, chunks[c]] = summed(1, k, c).astype(BF16)
        send_back(k, c, 0)

    def backward_end(k, h):
        low, high = h * half, (h + 1) * half
        if k:
            with jax.named_scope(f"ret_{k}_{h}"):
                rows = slice(low, high)
                whole(
                    pb.at[k, rows], ret_b.at[k, rows], ret_s.at[k - 1], ret_r.at[k - 1, h]
                ).wait_recv()
            pulled = ret_b[k, low:high].astype(F32)
        else:
            pulled = own_b[0, low:high]
            if h == 0:
                with jax.named_scope("red_b0"):
                    wait_near(1)
            for j in range(1, G):
                pulled = pulled + rpart_b[0, j, low:high].astype(F32)
        weighted = gates_b[k * C + low : k * C + high] * pulled * gain_ref[...]
        before = srt[k, low:high].astype(F32)
        inverse = lax.rsqrt(jnp.mean(before * before, axis=-1, keepdims=True) + epsilon)
        unit = before * inverse
        inner = jnp.mean(weighted * unit, axis=-1, keepdims=True)
        th[k, low:high] = (
            xs_b[k, low:high].astype(F32) + inverse * (weighted - unit * inner)
        ).astype(BF16)

    def send_end(k, h):
        rows = slice(h * half, (h + 1) * half)
        remote(th.at[k, rows], fin_b.at[k, rows], out_s.at[k], out_r.at[k], dev(-1, 0, 0))

    detour = pipes > 2 and halves > 1
    low_rows = slice(half, 2 * half)

    cut = tile_d * ((D * 5 // 7) // tile_d)
    by, direct = slice(0, cut), slice(cut, D)

    def by_way(target):
        return whole(via.at[:, by], fin_b.at[0, low_rows, by], via_s, out_r.at[0], target)

    def send_near(h):
        if h != 1 or not detour:
            send_end(0, h)
            return
        pl.when(s != 1)(lambda: send_end(0, h))

        @pl.when(s == 1)
        def _():
            remote(th.at[0, low_rows, by], via.at[:, by], out_s.at[0], via_r, dev(1, 0, 0))
            remote(
                th.at[0, low_rows, direct], fin_b.at[0, low_rows, direct],
                out_s.at[0], out_r.at[0], dev(-1, 0, 0),
            )

    def forward_via():
        if detour:
            @pl.when(s == 2)
            def _():
                whole(th.at[0, low_rows, by], via.at[:, by], out_s.at[0], via_r).wait_recv()
                by_way(dev(-2, 0, 0)).start()

    def forward_first(k, c):
        arrived(0, k, c)
        rows = rx_f[k, :, :, chunks[c]].astype(F32).reshape(G * C, -1)
        lanes = [rows[:, i : i + 128] for i in range(0, rows.shape[1], 128)]
        square = sum(lane * lane for lane in lanes)
        square_f[...] = square if c == 0 else square_f[...] + square
        scaled = (rows * gain_f[:, chunks[c]]).astype(BF16)
        for f in range(0, 2 * F, tile_f):
            hidden = dot(scaled, wi[chunks[c], f : f + tile_f])
            columns = slice(f, f + tile_f)
            sum_f[:, columns] = hidden if c == 0 else sum_f[:, columns] + hidden

    def forward_hidden():
        mean = jnp.sum(square_f[...], axis=-1, keepdims=True) * (1.0 / D)
        inverse = lax.rsqrt(mean + epsilon)
        for f in range(0, F, tile_f):
            gate = sum_f[:, f : f + tile_f] * inverse
            up = sum_f[:, F + f : F + f + tile_f] * inverse
            hidden_ref[:, f : f + tile_f] = (jax.nn.silu(gate) * up).astype(BF16)

    def forward_second(k, c):
        for d in range(chunks[c].start, chunks[c].stop, tile_d):
            columns = slice(d, d + tile_d)
            put_part(0, k, dot(hidden_ref[...], wo[:, columns]), columns)
        send_part(0, k, c)

    def forward_end(k, c):
        total = summed(0, k, c)
        moved = rx_f[k, 0, :, chunks[c]].astype(F32) + rg_f[k][:, :1] * total
        if k == 0:
            fin_f[0, :, chunks[c]] = moved.astype(BF16)
            return
        mv[k, :, chunks[c]] = moved.astype(BF16)
        remote(
            mv.at[k, :, chunks[c]], fin_f.at[k, :, chunks[c]],
            move_s.at[k - 1], move_r.at[k - 1], dev(0, -k, 0),
        )

    tile_f = tile_of(F, 256)
    with jax.named_scope("w_small"):
        for load in (load_gid, *load_small):
            load.wait()
    gather_f, scatter_f = placing(fid_ref[...], e, E, C, us_f.shape[1])
    gather_b, scatter_b = placing(gid_ref[...], e, E, C, us_b.shape[1])
    gather_f_rows, gather_b_rows = gather_f.astype(BF16), gather_b.astype(BF16)
    us_b[...] = scatter_b
    us_f[...] = scatter_f
    gates_b = jnp.sum(gather_b * ggate_ref[...], axis=1, keepdims=True)
    gates_f = jnp.sum(gather_f * fgate_ref[...], axis=1, keepdims=True)
    gs_f[...] = jnp.broadcast_to(gates_f, (T, gs_f.shape[2])).reshape(gs_f.shape)
    early = count // 2
    with jax.named_scope("w_x"):
        load_x.wait()
    for c in range(count):
        xs_f[:, :, chunks[c]] = (
            dot(gather_f_rows, x_ref[:, chunks[c]]).reshape(E, C, -1).astype(BF16)
        )
    with jax.named_scope("w_g"):
        load_g.wait()
    for c in range(count):
        rows = dot(gather_b_rows, g_ref[:, chunks[c]]).reshape(E, C, -1).astype(BF16)
        xs_b[:, :, chunks[c]] = rows
        rx_b[0, 0, :, chunks[c]] = rows[0]
    with jax.named_scope("w_bar"):
        pl.semaphore_wait(barrier, len(near) + E * (1 + (s + pipes - 1) // pipes))
    gain_copy = remote(gain_ref, gain_f, perm_s.at[2], perm_r.at[2], dev(1, 0, 0))
    for k in range(E):
        remote(gs_f.at[k], rg_f.at[k], gate_s, gate_r, dev(1, k, 0))
    perm_f = remote(us_f, ur_f, perm_s.at[0], perm_r.at[0], dev(1, 0, 0))

    def send_forward(order):
        for k, c in order:
            outgoing(0, k, c).start()

    far = [(k, c) for k in others for c in range(count)]
    own_rows = [(0, c) for c in range(count)]
    pl.when(s != pipes - 1)(lambda: send_forward(own_rows + far))
    pl.when(last)(lambda: send_forward(own_rows[-1:] + far + own_rows[:-1]))
    for c in range(count):
        for k in others:
            outgoing(1, k, c).start()
    for c in range(count):
        share(1, 0, c, xs_b.at[0, :, chunks[c]])
    pl.when(last)(lambda: greet(ready_sem, following))
    with jax.named_scope("w_saved"):
        load_saved.wait()
    srt[...] = dot(gather_b_rows, saved_ref[...]).reshape(E, C, D).astype(BF16)

    with jax.named_scope("w_wo"):
        load_wo.wait()
        load_acts.wait()
    with jax.named_scope("b1_0"):
        for c in range(count):
            backward_first(0, c)
        backward_hidden(0)
    with jax.named_scope("w_wi"):
        load_wi.wait()

    def near_end():
        whole(us_b, ur_b, perm_s.at[1], perm_r.at[1], dev(-1, 0, 0)).start()
        for h in range(halves):
            send_near(h)

    def last_ends():
        for k in others:
            for h in range(1, halves):
                with jax.named_scope(f"bend1_{h}"):
                    backward_end(k, h)
                    send_end(k, h)

    for c in range(count):
        with jax.named_scope(f"b2_0_{c}"):
            backward_second(0, c)
        if 1 <= c <= early:
            for k in others:
                pass_on(1, k, c - 1)
    for c in range(early):
        with jax.named_scope(f"b1_1a{c}"):
            backward_first(1, c)
        if c == 0:
            for k in others:
                for i in range(early, count - 1):
                    pass_on(1, k, i)
    for k in others:
        pass_on(1, k, count - 1)
    with jax.named_scope("bend0"):
        for h in range(halves):
            backward_end(0, h)
    for k in others:
        with jax.named_scope("b1_1b"):
            for c in range(early if k == 1 else 0, count):
                backward_first(k, c)
            backward_hidden(k)
        for c in range(count):
            with jax.named_scope(f"b2_1_{c}"):
                backward_second(k, c)
            if k == 1 and c == max(early - 1, 0):
                pl.when(s != 0)(near_end)
            if k == E - 1 and c >= early > 0:
                for other in others:
                    pass_on(0, other, c - early)
            if c >= 1:
                with jax.named_scope(f"bret_{c - 1}"):
                    backward_return(k, c - 1)
        if k == E - 1:
            for other in others:
                for c in range(early, count - 1):
                    pass_on(0, other, c)
        with jax.named_scope(f"bret_{count - 1}"):
            backward_return(k, count - 1)
        if k == E - 1:
            for other in others:
                pass_on(0, other, count - 1)
        for h in range(1, halves):
            for c in range(count):
                send_back(k, c, h)
    with jax.named_scope("w_gain"):
        gain_copy.wait_recv()
    with jax.named_scope("w_prev"):
        pl.when(first)(lambda: pl.semaphore_wait(ready_sem, E))
        pl.when(first)(near_end)
    with jax.named_scope("w_gate"):
        whole(gs_f, rg_f, gate_s, gate_r).wait_recv()
    for k in others:
        for c in range(count):
            with jax.named_scope(f"f1_1_{c}"):
                forward_first(k, c)
        with jax.named_scope("fh_1"):
            forward_hidden()
        if k == 1:
            with jax.named_scope("w_via"):
                forward_via()
        for c in range(count):
            with jax.named_scope(f"f2_1_{c}"):
                forward_second(k, c)
            if c == max(LAG, count - 2) or count == 1:
                with jax.named_scope("bend1_0"):
                    backward_end(k, 0)
                    send_end(k, 0)
            if c >= LAG:
                with jax.named_scope(f"fend_1_{c - LAG}"):
                    forward_end(k, c - LAG)
        if k == E - 1:
            for c in range(count):
                pass_on(0, 0, c)
        for c in range(max(count - LAG, 0), count):
            with jax.named_scope(f"fend_1_{c}"):
                forward_end(k, c)
    for c in range(count):
        with jax.named_scope(f"f1_0_{c}"):
            forward_first(0, c)
        if c == early - 1:
            last_ends()
    with jax.named_scope("fh_0"):
        forward_hidden()
    with jax.named_scope("f2_0"):
        for c in range(count):
            forward_second(0, c)
    if early == 0:
        last_ends()
    with jax.named_scope("fend0"):
        wait_near(0)
        for c in range(count):
            forward_end(0, c)

    with jax.named_scope("w_perm"):
        perm_f.wait_recv()
        whole(us_b, ur_b, perm_s.at[1], perm_r.at[1]).wait_recv()
    for k in others:
        with jax.named_scope("w_move"):
            whole(mv.at[k], fin_f.at[k], move_s.at[k - 1], move_r.at[k - 1]).wait_recv()
    for k in range(E):
        with jax.named_scope(f"w_out{k}"):
            whole(th.at[k], fin_b.at[k], out_s.at[k], out_r.at[k]).wait_recv()
    with jax.named_scope("w_sends"):
        for b in range(2):
            for k in range(b, E):
                i = b * (E - 1) + k
                whole(xs[b].at[k], rx[b].at[k, 0], disp_s.at[i], disp_r.at[i, 0]).wait_send()
            for k in range(E):
                for j in range(1, G):
                    i = (b, k, j - 1)
                    whole(
                        rx[b].at[k, 0], rx[b].at[k, j], relay_s.at[i], relay_r.at[(*i, 0)]
                    ).wait_send()
                    whole(part[b].at[k, j], rpart[b].at[k, j], red_s.at[i], near_r.at[b, j - 1]).wait_send()
        for k in others:
            whole(pb.at[k], ret_b.at[k], ret_s.at[k - 1], ret_r.at[k - 1, 0]).wait_send()
            whole(mv.at[k], fin_f.at[k], move_s.at[k - 1], move_r.at[k - 1]).wait_send()
        for k in range(E):
            whole(th.at[k], fin_b.at[k], out_s.at[k], out_r.at[k]).wait_send()
        whole(gs_f, rg_f, gate_s, gate_r).wait_send()
        if detour:
            pl.when(s == 2)(lambda: by_way(dev(-2, 0, 0)).wait_send())
        for copy in (gain_copy, perm_f, whole(us_b, ur_b, perm_s.at[1], perm_r.at[1])):
            copy.wait_send()


UNSORT_STEPS = 2


def unsort(fin_f, fin_b, ur_f, ur_b, fout_hbm, gout_hbm, held, sems):
    T, D = fout_hbm.shape
    width = D // UNSORT_STEPS
    copies = []
    for i, (fin, ur, out) in enumerate(((fin_f, ur_f, fout_hbm), (fin_b, ur_b, gout_hbm))):
        for c in range(UNSORT_STEPS):
            columns = pl.ds(c * width, width)
            rows = fin[:, :, columns].astype(F32).reshape(T, width).astype(BF16)
            held[i, :, columns] = dot(ur[:, :T], rows).astype(BF16)
            copy = pltpu.make_async_copy(held.at[i, :, columns], out.at[:, columns], sems.at[i, c])
            copy.start()
            copies.append(copy)
    for copy in copies:
        copy.wait()


def on_device(
    dims,
    forward_in,
    forward_ids,
    forward_gates,
    grad_in,
    grad_ids,
    grad_gates,
    saved_input,
    saved_acts,
    norm_gain,
    weight_in,
    weight_out,
):
    pipes, E, G = dims
    T, D = forward_in.shape[1:]
    F = weight_out.shape[1]
    C = T // E
    padded = -(-T // 128) * 128
    DMA = pltpu.SemaphoreType.DMA
    rows = (E, C, D)
    vmem = pl.BlockSpec(memory_space=pltpu.VMEM)
    hbm = pl.BlockSpec(memory_space=pl.ANY)
    sorted_rows = jax.ShapeDtypeStruct(rows, BF16)
    order = jax.ShapeDtypeStruct((T, padded), BF16)
    halves, N = disp_rows(C), len(columns_of(D, C))
    arrived = pl.pallas_call(
        functools.partial(kernel, dims),
        out_shape=(pltpu.VMEM(rows, BF16), pltpu.VMEM(rows, BF16), pltpu.VMEM((T, padded), BF16), pltpu.VMEM((T, padded), BF16)),
        in_specs=[hbm] * 11,
        out_specs=(vmem, vmem, vmem, vmem),
        scratch_shapes=[
            pltpu.VMEM((1, T), jnp.int32), pltpu.VMEM((1, T), F32),
            pltpu.VMEM((1, T), jnp.int32), pltpu.VMEM((1, T), F32),
            pltpu.VMEM((1, D), F32),
            pltpu.VMEM((T, D), BF16), pltpu.VMEM((T, D), BF16), pltpu.VMEM((T, D), BF16),
            pltpu.VMEM((E * G, C, 2 * F), BF16),
            pltpu.VMEM((D, 2 * F), BF16),
            pltpu.VMEM((F, D), BF16),
            pltpu.VMEM((1, D), F32),
            pltpu.VMEM(rows, BF16), pltpu.VMEM(rows, BF16),
            pltpu.VMEM((E, G, C, D), BF16), pltpu.VMEM((E, G, C, D), BF16),
            pltpu.VMEM((E, C, 128), F32), pltpu.VMEM((E, C, 128), F32),
            pltpu.VMEM((T, padded), BF16), pltpu.VMEM((T, padded), BF16),
            pltpu.VMEM((E, G, C, D), BF16), pltpu.VMEM((E, G, C, D), BF16),
            pltpu.VMEM((E, G, C, D), BF16), pltpu.VMEM((E, G, C, D), BF16),
            pltpu.VMEM(rows, F32), pltpu.VMEM(rows, F32),
            pltpu.VMEM(rows, BF16), pltpu.VMEM(rows, BF16), pltpu.VMEM(rows, BF16),
            pltpu.VMEM(rows, BF16), pltpu.VMEM(rows, BF16),
            pltpu.VMEM((G * C, F), BF16),
            pltpu.VMEM((G * C, 2 * F), BF16),
            pltpu.VMEM((G * C, F), F32), pltpu.VMEM((G * C, 2 * F), F32),
            pltpu.VMEM((G * C, 2 * F), F32), pltpu.VMEM((G * C, 128), F32),
            pltpu.VMEM((C // halves, D), BF16),
            DMA((11,)), pltpu.SemaphoreType.REGULAR, DMA, DMA,
            DMA((2 * E - 1,)), DMA((2 * E - 1, N)), DMA, DMA,
            DMA((2, E, G - 1)), DMA((2, E, G - 1, N)), DMA((3,)), DMA((3,)),
            DMA((2, E, G - 1)), DMA((2, E - 1, G - 1, N)), DMA((2, G - 1)),
            DMA((E - 1,)), DMA((E - 1,)), DMA((E,)), DMA((E,)),
            DMA((E - 1,)), DMA((E - 1, halves)),
        ],
        compiler_params=pltpu.CompilerParams(
            collective_id=0, has_side_effects=True, vmem_limit_bytes=40 * 2**20
        ),
    )(*[
        pltpu.with_memory_space_constraint(a, pltpu.HBM)
        for a in (
            forward_ids.reshape(1, T),
            forward_gates.reshape(1, T),
            grad_ids.reshape(1, T),
            grad_gates.reshape(1, T),
            norm_gain,
            forward_in[0],
            grad_in[0],
            saved_input[0],
            saved_acts.reshape(E * G, C, 2 * F),
            weight_in[0],
            weight_out[0],
        )
    ])
    out_shape = jax.ShapeDtypeStruct((T, D), BF16)
    fwd, grad = pl.pallas_call(
        unsort,
        out_shape=(out_shape, out_shape),
        in_specs=[vmem] * 4,
        out_specs=(hbm, hbm),
        scratch_shapes=[pltpu.VMEM((2, T, D), BF16), DMA((2, UNSORT_STEPS))],
        compiler_params=pltpu.CompilerParams(vmem_limit_bytes=8 * 2**20),
    )(*[pltpu.with_memory_space_constraint(a, pltpu.VMEM) for a in arrived])
    return fwd[None], grad[None]


def solution(mesh):
    sources = mesh.shape["expert"]
    G = min(4, sources // 2)
    dims = (mesh.shape["pipe"], sources // G, G)
    placed = (
        P("pipe", "expert", None),
        P("pipe", "expert", None),
        P("pipe", "expert", None),
        P("pipe", "expert", None),
        P("pipe", "expert", None),
        P("pipe", "expert", None),
        P("pipe", "expert", None),
        P("pipe", "expert", None, None),
        P("pipe", None),
        P("expert", None, None),
        P("expert", None, None),
    )
    return jax.shard_map(
        functools.partial(on_device, dims),
        mesh=mesh,
        in_specs=placed,
        out_specs=(P("pipe", "expert", None), P("pipe", "expert", None)),
        check_vma=False,
    )
```

time: 35.4 us -> 34.8 us (0.983)
  Pallas kernels: 34.6 us -> 34 us
    pallas_call x1, Pallas kernels: 33.5 us -> 32.9 us  [on_device(): pl.pallas_call(functools.partial(kernel, dims), out_shape=(pltpu.VMEM(row...]
where the time goes in v2:
time: 34.8 us; the launch traced here: 34.7 us
  Pallas kernels  34 us (98%)
  between operations  0.64 us (2%)
    pallas_call x1, Pallas kernels, on_device(): pl.pallas_call(functools.partial(kernel, dims), out_shape=(pltpu.VMEM(row...  32.9 us
    pallas_call x1, Pallas kernels, on_device(): pl.pallas_call(unsort, out_shape=(out_shape, out_shape), in_specs=[vmem]...  1.16 us

profile of v2, /device:TPU:0, one launch (start us, length us, event | category | flops | bytes accessed | tf_op | source)
XLA Modules:
  0.0 34.7 jit_solution(10808666993144356759)
XLA Ops:
  0.6 32.9 %shard_map.122 = (bf16[2,32,3584]{2,1,0:T(8,128)(2,1)S(1)}, bf16[2,32,3584]{2,1,0:T(8,128)(2,1)S(1)}, bf16[64,128]{1,0:T(8,128)(2,1)S(1)}, bf16[64,128]{1,0:T(8,128)(2,1)S(1)}) custom-call(s32[1,64]{1,0:T(1,128)} %bitcast.18, f32[1,64]{1,0:T(1,128)} %bitcast.19, s32[1,64]{1,0:T(1,128)} %bitcast.20, f32[1,64]{1,0:T(1,128)} %bitcast.21, f32[1,3584]{1,0:T(1,128)} %gain_hbm.1, ...), custom_call_target="tpu_custom_call" | custom-call | tf_op jit(solution)/shard_map/pallas_call | solution.py:580
  33.5 1.2 %shard_map.123 = (bf16[64,3584]{1,0:T(8,128)(2,1)}, bf16[64,3584]{1,0:T(8,128)(2,1)}) custom-call(bf16[2,32,3584]{2,1,0:T(8,128)(2,1)S(1)} %get-tuple-element.8.fin_f, bf16[2,32,3584]{2,1,0:T(8,128)(2,1)S(1)} %get-tuple-element.9.fin_b, bf16[64,128]{1,0:T(8,128)(2,1)S(1)} %get-tuple-element.10.ur_f, bf16[64,128]{1,0:T(8,128)(2,1)S(1)} %get-tuple-element.11.ur_b), custom_call_target="tpu_custom_call" | custom-call | tf_op jit(solution)/shard_map/pallas_call | solution.py:635

commit v3 on v2

--- a/solution.py
+++ b/solution.py
@@ -1,3 +1,4 @@
+import contextlib
 import functools
 
 import jax
@@ -11,6 +12,13 @@
 F32 = jnp.float32
 BF16 = jnp.bfloat16
 MESH = pl.DeviceIdType.MESH
+
+
+@contextlib.contextmanager
+def stage(name):
+    with jax.named_scope(name):
+        pl.delay(1)
+        yield
 
 
 def tile_of(width, most):
@@ -238,7 +246,7 @@
     def backward_end(k, h):
         low, high = h * half, (h + 1) * half
         if k:
-            with jax.named_scope(f"ret_{k}_{h}"):
+            with stage(f"ret_{k}_{h}"):
                 rows = slice(low, high)
                 whole(
                     pb.at[k, rows], ret_b.at[k, rows], ret_s.at[k - 1], ret_r.at[k - 1, h]
@@ -385,7 +393,7 @@
     with jax.named_scope("w_wo"):
         load_wo.wait()
         load_acts.wait()
-    with jax.named_scope("b1_0"):
+    with stage("b1_0"):
         for c in range(count):
             backward_first(0, c)
         backward_hidden(0)
@@ -400,18 +408,18 @@
     def last_ends():
         for k in others:
             for h in range(1, halves):
-                with jax.named_scope(f"bend1_{h}"):
+                with stage(f"bend1_{h}"):
                     backward_end(k, h)
                     send_end(k, h)
 
     for c in range(count):
-        with jax.named_scope(f"b2_0_{c}"):
+        with stage(f"b2_0_{c}"):
             backward_second(0, c)
         if 1 <= c <= early:
             for k in others:
                 pass_on(1, k, c - 1)
     for c in range(early):
-        with jax.named_scope(f"b1_1a{c}"):
+        with stage(f"b1_1a{c}"):
             backward_first(1, c)
         if c == 0:
             for k in others:
@@ -419,16 +427,16 @@
                     pass_on(1, k, i)
     for k in others:
         pass_on(1, k, count - 1)
-    with jax.named_scope("bend0"):
+    with stage("bend0"):
         for h in range(halves):
             backward_end(0, h)
     for k in others:
-        with jax.named_scope("b1_1b"):
+        with stage("b1_1b"):
             for c in range(early if k == 1 else 0, count):
                 backward_first(k, c)
             backward_hidden(k)
         for c in range(count):
-            with jax.named_scope(f"b2_1_{c}"):
+            with stage(f"b2_1_{c}"):
                 backward_second(k, c)
             if k == 1 and c == max(early - 1, 0):
                 pl.when(s != 0)(near_end)
@@ -436,13 +444,13 @@
                 for other in others:
                     pass_on(0, other, c - early)
             if c >= 1:
-                with jax.named_scope(f"bret_{c - 1}"):
+                with stage(f"bret_{c - 1}"):
                     backward_return(k, c - 1)
         if k == E - 1:
             for other in others:
                 for c in range(early, count - 1):
                     pass_on(0, other, c)
-        with jax.named_scope(f"bret_{count - 1}"):
+        with stage(f"bret_{count - 1}"):
             backward_return(k, count - 1)
         if k == E - 1:
             for other in others:
@@ -459,42 +467,42 @@
         whole(gs_f, rg_f, gate_s, gate_r).wait_recv()
     for k in others:
         for c in range(count):
-            with jax.named_scope(f"f1_1_{c}"):
+            with stage(f"f1_1_{c}"):
                 forward_first(k, c)
-        with jax.named_scope("fh_1"):
+        with stage("fh_1"):
             forward_hidden()
         if k == 1:
             with jax.named_scope("w_via"):
                 forward_via()
         for c in range(count):
-            with jax.named_scope(f"f2_1_{c}"):
+            with stage(f"f2_1_{c}"):
                 forward_second(k, c)
             if c == max(LAG, count - 2) or count == 1:
-                with jax.named_scope("bend1_0"):
+                with stage("bend1_0"):
                     backward_end(k, 0)
                     send_end(k, 0)
             if c >= LAG:
-                with jax.named_scope(f"fend_1_{c - LAG}"):
+                with stage(f"fend_1_{c - LAG}"):
                     forward_end(k, c - LAG)
         if k == E - 1:
             for c in range(count):
                 pass_on(0, 0, c)
         for c in range(max(count - LAG, 0), count):
-            with jax.named_scope(f"fend_1_{c}"):
+            with stage(f"fend_1_{c}"):
                 forward_end(k, c)
     for c in range(count):
-        with jax.named_scope(f"f1_0_{c}"):
+        with stage(f"f1_0_{c}"):
             forward_first(0, c)
         if c == early - 1:
             last_ends()
-    with jax.named_scope("fh_0"):
+    with stage("fh_0"):
         forward_hidden()
-    with jax.named_scope("f2_0"):
+    with stage("f2_0"):
         for c in range(count):
             forward_second(0, c)
     if early == 0:
         last_ends()
-    with jax.named_scope("fend0"):
+    with stage("fend0"):
         wait_near(0)
         for c in range(count):
             forward_end(0, c)

time: 34.8 us -> 30.8 us (0.89)
  Pallas kernels: 34 us -> 30 us
    pallas_call x1, Pallas kernels: 32.9 us -> 28.9 us  [on_device(): pl.pallas_call(functools.partial(kernel, dims), out_shape=(pltpu.VMEM(row...]
where the time goes in v3:
time: 30.8 us; the launch traced here: 30.7 us
  Pallas kernels  30 us (97%)
  between operations  0.64 us (2%)
    pallas_call x1, Pallas kernels, on_device(): pl.pallas_call(functools.partial(kernel, dims), out_shape=(pltpu.VMEM(row...  28.9 us
    pallas_call x1, Pallas kernels, on_device(): pl.pallas_call(unsort, out_shape=(out_shape, out_shape), in_specs=[vmem]...  1.16 us

profile of v3, /device:TPU:0, one launch (start us, length us, event | category | flops | bytes accessed | tf_op | source)
XLA Modules:
  0.0 30.7 jit_solution(4403272068159745326)
XLA Ops:
  0.6 28.9 %shard_map.122 = (bf16[2,32,3584]{2,1,0:T(8,128)(2,1)S(1)}, bf16[2,32,3584]{2,1,0:T(8,128)(2,1)S(1)}, bf16[64,128]{1,0:T(8,128)(2,1)S(1)}, bf16[64,128]{1,0:T(8,128)(2,1)S(1)}) custom-call(s32[1,64]{1,0:T(1,128)} %bitcast.18, f32[1,64]{1,0:T(1,128)} %bitcast.19, s32[1,64]{1,0:T(1,128)} %bitcast.20, f32[1,64]{1,0:T(1,128)} %bitcast.21, f32[1,3584]{1,0:T(1,128)} %gain_hbm.1, ...), custom_call_target="tpu_custom_call" | custom-call | tf_op jit(solution)/shard_map/pallas_call | solution.py:588
  29.5 1.2 %shard_map.123 = (bf16[64,3584]{1,0:T(8,128)(2,1)}, bf16[64,3584]{1,0:T(8,128)(2,1)}) custom-call(bf16[2,32,3584]{2,1,0:T(8,128)(2,1)S(1)} %get-tuple-element.8.fin_f, bf16[2,32,3584]{2,1,0:T(8,128)(2,1)S(1)} %get-tuple-element.9.fin_b, bf16[64,128]{1,0:T(8,128)(2,1)S(1)} %get-tuple-element.10.ur_f, bf16[64,128]{1,0:T(8,128)(2,1)S(1)} %get-tuple-element.11.ur_b), custom_call_target="tpu_custom_call" | custom-call | tf_op jit(solution)/shard_map/pallas_call | solution.py:643

commit v4 on v3

--- a/solution.py
+++ b/solution.py
@@ -78,7 +78,7 @@
     xs_f, xs_b, rx_f, rx_b, gs_f, rg_f, us_f, us_b,
     part_f, part_b, rpart_f, rpart_b, own_f, own_b,
     mv, pb, ret_b, th, srt, hidden_ref, joined, sum_b, both_b, sum_f, square_f,
-    via, w_sem, ready_sem, via_s, via_r,
+    via, w_sem, ready_sem, side_sem, via_s, via_r,
     disp_s, disp_r, gate_s, gate_r, relay_s, relay_r, perm_s, perm_r, red_s, red_r, near_r,
     move_s, move_r, out_s, out_r, ret_s, ret_r,
 ):
@@ -98,8 +98,8 @@
         )
 
     near = [dev(0, k, 0) for k in range(1, E)] + [dev(0, 0, j) for j in range(1, G)]
-    following = [dev(1, k, 0) for k in range(E)]
-    previous = [dev(-1, k, 0) for k in range(E)]
+    beside = [dev(0, k, 0) for k in range(1, E)]
+    following, previous = [dev(1, 0, 0)], [dev(-1, 0, 0)]
     first, last = s == 0, s == pipes - 1
 
     def greet(sem, peers):
@@ -359,6 +359,20 @@
         xs_f[:, :, chunks[c]] = (
             dot(gather_f_rows, x_ref[:, chunks[c]]).reshape(E, C, -1).astype(BF16)
         )
+    arrivals = len(near) + 1 + (s + pipes - 1) // pipes
+
+    def send_forward(order):
+        for k, c in order:
+            outgoing(0, k, c).start()
+
+    far = [(k, c) for k in others for c in range(count)]
+    own_rows = [(0, c) for c in range(count)]
+
+    @pl.when(last)
+    def _():
+        pl.semaphore_wait(barrier, arrivals)
+        send_forward(own_rows[-1:])
+
     with jax.named_scope("w_g"):
         load_g.wait()
     for c in range(count):
@@ -366,20 +380,13 @@
         xs_b[:, :, chunks[c]] = rows
         rx_b[0, 0, :, chunks[c]] = rows[0]
     with jax.named_scope("w_bar"):
-        pl.semaphore_wait(barrier, len(near) + E * (1 + (s + pipes - 1) // pipes))
+        pl.when(s != pipes - 1)(lambda: pl.semaphore_wait(barrier, arrivals))
     gain_copy = remote(gain_ref, gain_f, perm_s.at[2], perm_r.at[2], dev(1, 0, 0))
-    for k in range(E):
-        remote(gs_f.at[k], rg_f.at[k], gate_s, gate_r, dev(1, k, 0))
+    remote(gs_f.at[0], rg_f.at[0], gate_s, gate_r, dev(1, 0, 0))
     perm_f = remote(us_f, ur_f, perm_s.at[0], perm_r.at[0], dev(1, 0, 0))
 
-    def send_forward(order):
-        for k, c in order:
-            outgoing(0, k, c).start()
-
-    far = [(k, c) for k in others for c in range(count)]
-    own_rows = [(0, c) for c in range(count)]
-    pl.when(s != pipes - 1)(lambda: send_forward(own_rows + far))
-    pl.when(last)(lambda: send_forward(own_rows[-1:] + far + own_rows[:-1]))
+    greet(side_sem, beside)
+    pl.when(s != pipes - 1)(lambda: send_forward(own_rows))
     for c in range(count):
         for k in others:
             outgoing(1, k, c).start()
@@ -389,6 +396,12 @@
     with jax.named_scope("w_saved"):
         load_saved.wait()
     srt[...] = dot(gather_b_rows, saved_ref[...]).reshape(E, C, D).astype(BF16)
+    with stage("w_side"):
+        pl.semaphore_wait(side_sem, len(beside))
+    for k in others:
+        remote(gs_f.at[k], rg_f.at[k], gate_s, gate_r, dev(1, k, 0))
+    send_forward(far)
+    pl.when(last)(lambda: send_forward(own_rows[:-1]))
 
     with jax.named_scope("w_wo"):
         load_wo.wait()
@@ -438,7 +451,7 @@
         for c in range(count):
             with stage(f"b2_1_{c}"):
                 backward_second(k, c)
-            if k == 1 and c == max(early - 1, 0):
+            if k == 1 and c == min(2, count - 1):
                 pl.when(s != 0)(near_end)
             if k == E - 1 and c >= early > 0:
                 for other in others:
@@ -461,7 +474,7 @@
     with jax.named_scope("w_gain"):
         gain_copy.wait_recv()
     with jax.named_scope("w_prev"):
-        pl.when(first)(lambda: pl.semaphore_wait(ready_sem, E))
+        pl.when(first)(lambda: pl.semaphore_wait(ready_sem, 1))
         pl.when(first)(near_end)
     with jax.named_scope("w_gate"):
         whole(gs_f, rg_f, gate_s, gate_r).wait_recv()
@@ -613,7 +626,7 @@
             pltpu.VMEM((G * C, F), F32), pltpu.VMEM((G * C, 2 * F), F32),
             pltpu.VMEM((G * C, 2 * F), F32), pltpu.VMEM((G * C, 128), F32),
             pltpu.VMEM((C // halves, D), BF16),
-            DMA((11,)), pltpu.SemaphoreType.REGULAR, DMA, DMA,
+            DMA((11,)), pltpu.SemaphoreType.REGULAR, pltpu.SemaphoreType.REGULAR, DMA, DMA,
             DMA((2 * E - 1,)), DMA((2 * E - 1, N)), DMA, DMA,
             DMA((2, E, G - 1)), DMA((2, E, G - 1, N)), DMA((3,)), DMA((3,)),
             DMA((2, E, G - 1)), DMA((2, E - 1, G - 1, N)), DMA((2, G - 1)),

time: 30.8 us -> 30.6 us (level)
  no operation moved by 1% of the time
where the time goes in v4:
time: 30.6 us; the launch traced here: 30.4 us
  Pallas kernels  29.8 us (97%)
  between operations  0.64 us (2%)
    pallas_call x1, Pallas kernels, on_device(): pl.pallas_call(functools.partial(kernel, dims), out_shape=(pltpu.VMEM(row...  28.6 us
    pallas_call x1, Pallas kernels, on_device(): pl.pallas_call(unsort, out_shape=(out_shape, out_shape), in_specs=[vmem]...  1.17 us

profile of v4, /device:TPU:0, one launch (start us, length us, event | category | flops | bytes accessed | tf_op | source)
XLA Modules:
  0.0 30.4 jit_solution(13422551932996960819)
XLA Ops:
  0.6 28.6 %shard_map.122 = (bf16[2,32,3584]{2,1,0:T(8,128)(2,1)S(1)}, bf16[2,32,3584]{2,1,0:T(8,128)(2,1)S(1)}, bf16[64,128]{1,0:T(8,128)(2,1)S(1)}, bf16[64,128]{1,0:T(8,128)(2,1)S(1)}) custom-call(s32[1,64]{1,0:T(1,128)} %bitcast.18, f32[1,64]{1,0:T(1,128)} %bitcast.19, s32[1,64]{1,0:T(1,128)} %bitcast.20, f32[1,64]{1,0:T(1,128)} %bitcast.21, f32[1,3584]{1,0:T(1,128)} %gain_hbm.1, ...), custom_call_target="tpu_custom_call" | custom-call | tf_op jit(solution)/shard_map/pallas_call | solution.py:601
  29.3 1.2 %shard_map.123 = (bf16[64,3584]{1,0:T(8,128)(2,1)}, bf16[64,3584]{1,0:T(8,128)(2,1)}) custom-call(bf16[2,32,3584]{2,1,0:T(8,128)(2,1)S(1)} %get-tuple-element.8.fin_f, bf16[2,32,3584]{2,1,0:T(8,128)(2,1)S(1)} %get-tuple-element.9.fin_b, bf16[64,128]{1,0:T(8,128)(2,1)S(1)} %get-tuple-element.10.ur_f, bf16[64,128]{1,0:T(8,128)(2,1)S(1)} %get-tuple-element.11.ur_b), custom_call_target="tpu_custom_call" | custom-call | tf_op jit(solution)/shard_map/pallas_call | solution.py:656

commit v5 on v4

--- a/solution.py
+++ b/solution.py
@@ -80,6 +80,7 @@
     mv, pb, ret_b, th, srt, hidden_ref, joined, sum_b, both_b, sum_f, square_f,
     via, w_sem, ready_sem, side_sem, via_s, via_r,
     disp_s, disp_r, gate_s, gate_r, relay_s, relay_r, perm_s, perm_r, red_s, red_r, near_r,
+    row_r, same_r,
     move_s, move_r, out_s, out_r, ret_s, ret_r,
 ):
     pipes, E, G = dims
@@ -156,7 +157,7 @@
     def outgoing(b, k, c):
         return pltpu.make_async_remote_copy(
             src_ref=xs[b].at[k, :, chunks[c]], dst_ref=rx[b].at[k, 0, :, chunks[c]],
-            send_sem=disp_s.at[b * (E - 1) + k], recv_sem=disp_r.at[b * (E - 1) + k, c],
+            send_sem=disp_s.at[b], recv_sem=disp_r.at[b, k - 1, c] if k else row_r,
             device_id=dev(1 - b, k, 0), device_id_type=MESH,
         )
 
@@ -164,8 +165,13 @@
         for j in range(1, G):
             relay[b, k, j, c] = remote(
                 source, rx[b].at[k, j, :, chunks[c]],
-                relay_s.at[b, k, j - 1], relay_r.at[b, k, j - 1, c], dev(0, 0, j),
+                relay_s.at[b, j - 1], relay_r.at[b, k - 1, j - 1, c], dev(0, 0, j),
             )
+
+    def same(b, j, source):
+        return whole(
+            source, rx[b].at[0, j], relay_s.at[b, j - 1], same_r.at[b, j - 1], dev(0, 0, j)
+        )
 
     def pass_on(b, k, c):
         with jax.named_scope(f"pass_{b}_{k}_{c}"):
@@ -175,7 +181,10 @@
     def arrived(b, k, c):
         with jax.named_scope(f"arr_{b}_{k}_{c}"):
             for j in range(1, G):
-                relay[b, k, j, c].wait_recv()
+                if k:
+                    relay[b, k, j, c].wait_recv()
+                elif c == 0:
+                    same(b, j, xs[b].at[0]).wait_recv()
 
     def put_part(b, k, rows, columns):
         rows = rows.reshape(G, C, rows.shape[-1])
@@ -187,7 +196,7 @@
         for j in range(1, G):
             reduce[b, k, j, c] = remote(
                 part[b].at[k, j, :, chunks[c]], rpart[b].at[k, j, :, chunks[c]],
-                red_s.at[b, k, j - 1], landed(b, k, j, c), dev(0, 0, j),
+                red_s.at[b, j - 1], landed(b, k, j, c), dev(0, 0, j),
             )
 
     def landed(b, k, j, c):
@@ -196,7 +205,7 @@
     def wait_near(b):
         for j in range(1, G):
             whole(
-                part[b].at[0, j], rpart[b].at[0, j], red_s.at[b, 0, j - 1], near_r.at[b, j - 1]
+                part[b].at[0, j], rpart[b].at[0, j], red_s.at[b, j - 1], near_r.at[b, j - 1]
             ).wait_recv()
 
     def summed(b, k, c):
@@ -270,7 +279,7 @@
 
     def send_end(k, h):
         rows = slice(h * half, (h + 1) * half)
-        remote(th.at[k, rows], fin_b.at[k, rows], out_s.at[k], out_r.at[k], dev(-1, 0, 0))
+        remote(th.at[k, rows], fin_b.at[k, rows], out_s, out_r, dev(-1, 0, 0))
 
     detour = pipes > 2 and halves > 1
     low_rows = slice(half, 2 * half)
@@ -279,7 +288,7 @@
     by, direct = slice(0, cut), slice(cut, D)
 
     def by_way(target):
-        return whole(via.at[:, by], fin_b.at[0, low_rows, by], via_s, out_r.at[0], target)
+        return whole(via.at[:, by], fin_b.at[0, low_rows, by], via_s, out_r, target)
 
     def send_near(h):
         if h != 1 or not detour:
@@ -289,17 +298,17 @@
 
         @pl.when(s == 1)
         def _():
-            remote(th.at[0, low_rows, by], via.at[:, by], out_s.at[0], via_r, dev(1, 0, 0))
+            remote(th.at[0, low_rows, by], via.at[:, by], out_s, via_r, dev(1, 0, 0))
             remote(
                 th.at[0, low_rows, direct], fin_b.at[0, low_rows, direct],
-                out_s.at[0], out_r.at[0], dev(-1, 0, 0),
+                out_s, out_r, dev(-1, 0, 0),
             )
 
     def forward_via():
         if detour:
             @pl.when(s == 2)
             def _():
-                whole(th.at[0, low_rows, by], via.at[:, by], out_s.at[0], via_r).wait_recv()
+                whole(th.at[0, low_rows, by], via.at[:, by], out_s, via_r).wait_recv()
                 by_way(dev(-2, 0, 0)).start()
 
     def forward_first(k, c):
@@ -390,8 +399,8 @@
     for c in range(count):
         for k in others:
             outgoing(1, k, c).start()
-    for c in range(count):
-        share(1, 0, c, xs_b.at[0, :, chunks[c]])
+    for j in range(1, G):
+        same(1, j, xs_b.at[0]).start()
     pl.when(last)(lambda: greet(ready_sem, following))
     with jax.named_scope("w_saved"):
         load_saved.wait()
@@ -498,8 +507,10 @@
                 with stage(f"fend_1_{c - LAG}"):
                     forward_end(k, c - LAG)
         if k == E - 1:
-            for c in range(count):
-                pass_on(0, 0, c)
+            with jax.named_scope("pass_0_0"):
+                whole(xs_f.at[0], rx_f.at[0, 0], disp_s.at[0], row_r).wait_recv()
+            for j in range(1, G):
+                same(0, j, rx_f.at[0, 0]).start()
         for c in range(max(count - LAG, 0), count):
             with stage(f"fend_1_{c}"):
                 forward_end(k, c)
@@ -526,26 +537,19 @@
     for k in others:
         with jax.named_scope("w_move"):
             whole(mv.at[k], fin_f.at[k], move_s.at[k - 1], move_r.at[k - 1]).wait_recv()
-    for k in range(E):
-        with jax.named_scope(f"w_out{k}"):
-            whole(th.at[k], fin_b.at[k], out_s.at[k], out_r.at[k]).wait_recv()
+    with jax.named_scope("w_out"):
+        whole(th, fin_b, out_s, out_r).wait_recv()
     with jax.named_scope("w_sends"):
         for b in range(2):
-            for k in range(b, E):
-                i = b * (E - 1) + k
-                whole(xs[b].at[k], rx[b].at[k, 0], disp_s.at[i], disp_r.at[i, 0]).wait_send()
-            for k in range(E):
-                for j in range(1, G):
-                    i = (b, k, j - 1)
-                    whole(
-                        rx[b].at[k, 0], rx[b].at[k, j], relay_s.at[i], relay_r.at[(*i, 0)]
-                    ).wait_send()
-                    whole(part[b].at[k, j], rpart[b].at[k, j], red_s.at[i], near_r.at[b, j - 1]).wait_send()
+            rows = xs[b].at[pl.ds(b, E - b)]
+            whole(rows, rows, disp_s.at[b], row_r).wait_send()
+            for j in range(1, G):
+                for sem in (relay_s, red_s):
+                    whole(xs[b], xs[b], sem.at[b, j - 1], row_r).wait_send()
         for k in others:
             whole(pb.at[k], ret_b.at[k], ret_s.at[k - 1], ret_r.at[k - 1, 0]).wait_send()
             whole(mv.at[k], fin_f.at[k], move_s.at[k - 1], move_r.at[k - 1]).wait_send()
-        for k in range(E):
-            whole(th.at[k], fin_b.at[k], out_s.at[k], out_r.at[k]).wait_send()
+        whole(th, fin_b, out_s, out_r).wait_send()
         whole(gs_f, rg_f, gate_s, gate_r).wait_send()
         if detour:
             pl.when(s == 2)(lambda: by_way(dev(-2, 0, 0)).wait_send())
@@ -627,10 +631,11 @@
             pltpu.VMEM((G * C, 2 * F), F32), pltpu.VMEM((G * C, 128), F32),
             pltpu.VMEM((C // halves, D), BF16),
             DMA((11,)), pltpu.SemaphoreType.REGULAR, pltpu.SemaphoreType.REGULAR, DMA, DMA,
-            DMA((2 * E - 1,)), DMA((2 * E - 1, N)), DMA, DMA,
-            DMA((2, E, G - 1)), DMA((2, E, G - 1, N)), DMA((3,)), DMA((3,)),
-            DMA((2, E, G - 1)), DMA((2, E - 1, G - 1, N)), DMA((2, G - 1)),
-            DMA((E - 1,)), DMA((E - 1,)), DMA((E,)), DMA((E,)),
+            DMA((2,)), DMA((2, E - 1, N)), DMA, DMA,
+            DMA((2, G - 1)), DMA((2, E - 1, G - 1, N)), DMA((3,)), DMA((3,)),
+            DMA((2, G - 1)), DMA((2, E - 1, G - 1, N)), DMA((2, G - 1)),
+            DMA, DMA((2, G - 1)),
+            DMA((E - 1,)), DMA((E - 1,)), DMA, DMA,
             DMA((E - 1,)), DMA((E - 1, halves)),
         ],
         compiler_params=pltpu.CompilerParams(

time: 30.6 us -> 30.4 us (level)
  no operation moved by 1% of the time
where the time goes in v5:
time: 30.4 us; the launch traced here: 30.3 us
  Pallas kernels  29.7 us (98%)
  between operations  0.64 us (2%)
    pallas_call x1, Pallas kernels, on_device(): pl.pallas_call(functools.partial(kernel, dims), out_shape=(pltpu.VMEM(row...  28.5 us
    pallas_call x1, Pallas kernels, on_device(): pl.pallas_call(unsort, out_shape=(out_shape, out_shape), in_specs=[vmem]...  1.17 us

profile of v5, /device:TPU:0, one launch (start us, length us, event | category | flops | bytes accessed | tf_op | source)
XLA Modules:
  0.0 30.3 jit_solution(4283678009549543436)
XLA Ops:
  0.6 28.5 %shard_map.122 = (bf16[2,32,3584]{2,1,0:T(8,128)(2,1)S(1)}, bf16[2,32,3584]{2,1,0:T(8,128)(2,1)S(1)}, bf16[64,128]{1,0:T(8,128)(2,1)S(1)}, bf16[64,128]{1,0:T(8,128)(2,1)S(1)}) custom-call(s32[1,64]{1,0:T(1,128)} %bitcast.18, f32[1,64]{1,0:T(1,128)} %bitcast.19, s32[1,64]{1,0:T(1,128)} %bitcast.20, f32[1,64]{1,0:T(1,128)} %bitcast.21, f32[1,3584]{1,0:T(1,128)} %gain_hbm.1, ...), custom_call_target="tpu_custom_call" | custom-call | tf_op jit(solution)/shard_map/pallas_call | solution.py:605
  29.1 1.2 %shard_map.123 = (bf16[64,3584]{1,0:T(8,128)(2,1)}, bf16[64,3584]{1,0:T(8,128)(2,1)}) custom-call(bf16[2,32,3584]{2,1,0:T(8,128)(2,1)S(1)} %get-tuple-element.8.fin_f, bf16[2,32,3584]{2,1,0:T(8,128)(2,1)S(1)} %get-tuple-element.9.fin_b, bf16[64,128]{1,0:T(8,128)(2,1)S(1)} %get-tuple-element.10.ur_f, bf16[64,128]{1,0:T(8,128)(2,1)S(1)} %get-tuple-element.11.ur_b), custom_call_target="tpu_custom_call" | custom-call | tf_op jit(solution)/shard_map/pallas_call | solution.py:661
